TPU v7x, 128 devices: a whole 4x4x4 slice. The times are simulated.
128 devices in a mesh: batch: 1, outer: 2 (over core), rows: 64 (over z, y, x).
Axes of the slice: x: 4, y: 4, z: 4, core: 2. Of those that a mesh axis runs over, the one named last changes fastest.
Arguments:
- a_mat: float32 [131072, 768], P(('batch', 'outer', 'rows'))
Outputs:
- output 1: float32 [131072, 768], P(('batch', 'outer', 'rows'))
- output 2: float32 [768, 768], P('batch')
All inputs are finite; a program needn't handle non-finite values.
Results may differ from a plain program's by a relative error of at most 0.001.
Values sent between devices are 32-bit elements.
A program may use at most 1 GiB of HBM per device.

v0:
```python
import jax
import jax.numpy as jnp
from jax import lax
from jax.sharding import PartitionSpec as P

FULL_PREC = lax.Precision.HIGHEST
GROUP_AXES = ("outer", "rows")


def sweep_local(row_blk):
    part_gram = lax.dot_general(row_blk, row_blk, (((0,), (0,)), ((), ())), precision=FULL_PREC, preferred_element_type=jnp.float32)
    gram_mat = lax.psum(part_gram, GROUP_AXES)
    low_fac = jnp.linalg.cholesky(gram_mat)
    solved = lax.linalg.triangular_solve(low_fac, row_blk, left_side=False, lower=True, transpose_a=True)
    return solved, low_fac


def solution(mesh):
    row_spec = P(("batch", "outer", "rows"), None)

    def local_qr(row_blk):
        q_one, low_one = sweep_local(row_blk)
        q_two, low_two = sweep_local(q_one)
        r_fac = lax.dot_general(low_two, low_one, (((0,), (1,)), ((), ())), precision=FULL_PREC, preferred_element_type=jnp.float32)
        return q_two, r_fac

    return jax.shard_map(local_qr, mesh=mesh, in_specs=(row_spec,), out_specs=(row_spec, P("batch", None)), check_vma=False)
```

profile of v0, /device:TPU:1, one launch (start us, length us, event | category | flops | bytes accessed | tf_op | source)
XLA Modules:
  0.0 873.5 jit_solution(18121625247062831191)
XLA Ops:
  7.2 11.6 %fusion.142 = f32[768,768]{0,1:T(8,128)} fusion(f32[1024,768]{1,0:T(8,128)} %param.4), kind=kOutput, calls=%fused_computation.240 | convolution fusion | flops 7247757312 | bytes 5505024 | tf_op jit(solution)/shard_map/dot_general | solution.py:11
  18.9 155.3 %all-reduce.4.cloned.1.call-done = f32[768,768]{0,1:T(8,128)} async-done(((f32[768,768]{0,1:T(8,128)}), f32[768,768]{0,1:T(8,128)}) %all-reduce.4.cloned.1.call-update) | async-done | bytes 2359312 | tf_op jit(solution)/shard_map/psum | solution.py:12
  180.9 11.7 %cholesky.453 = f32[128,128]{1,0:T(8,128)S(1)} custom-call(f32[128,128]{1,0:T(8,128)S(1)} %cholesky.669), custom_call_target="Cholesky" | custom-call | tf_op jit(solution)/shard_map/jit(cholesky)/cholesky | solution.py:13
  192.7 9.8 %custom-call.41 = f32[1,128,128]{1,2,0:T(8,128)S(1)} custom-call(f32[1,128,128]{2,1,0:T(8,128)S(1)} %get-tuple-element.93), custom_call_target="InvertDiagBlocksLowerTriangular" | custom-call | tf_op jit(solution)/shard_map/jit(cholesky)/cholesky | solution.py:13
  205.5 11.7 %cholesky.472 = f32[128,128]{1,0:T(8,128)S(1)} custom-call(f32[128,128]{1,0:T(8,128)S(1)} %cholesky.673), custom_call_target="Cholesky" | custom-call | tf_op jit(solution)/shard_map/jit(cholesky)/cholesky | solution.py:13
  217.2 10.0 %custom-call.42 = f32[1,128,128]{1,2,0:T(8,128)S(1)} custom-call(f32[1,128,128]{2,1,0:T(8,128)S(1)} %get-tuple-element.90), custom_call_target="InvertDiagBlocksLowerTriangular" | custom-call | tf_op jit(solution)/shard_map/jit(cholesky)/cholesky | solution.py:13
  229.1 11.7 %cholesky.493 = f32[128,128]{1,0:T(8,128)S(1)} custom-call(f32[128,128]{1,0:T(8,128)S(1)} %cholesky.678), custom_call_target="Cholesky" | custom-call | tf_op jit(solution)/shard_map/jit(cholesky)/cholesky | solution.py:13
  241.6 9.8 %custom-call.43 = f32[1,128,128]{1,2,0:T(8,128)S(1)} custom-call(f32[1,128,128]{2,1,0:T(8,128)S(1)} %get-tuple-element.87), custom_call_target="InvertDiagBlocksLowerTriangular" | custom-call | tf_op jit(solution)/shard_map/jit(cholesky)/cholesky | solution.py:13
  253.3 12.2 %cholesky.512 = f32[128,128]{1,0:T(8,128)S(1)} custom-call(f32[128,128]{1,0:T(8,128)S(1)} %cholesky.683), custom_call_target="Cholesky" | custom-call | tf_op jit(solution)/shard_map/jit(cholesky)/cholesky | solution.py:13
  266.2 9.8 %custom-call.44 = f32[1,128,128]{1,2,0:T(8,128)S(1)} custom-call(f32[1,128,128]{2,1,0:T(8,128)S(1)} %get-tuple-element.84), custom_call_target="InvertDiagBlocksLowerTriangular" | custom-call | tf_op jit(solution)/shard_map/jit(cholesky)/cholesky | solution.py:13
  277.7 11.7 %cholesky.531 = f32[128,128]{1,0:T(8,128)S(1)} custom-call(f32[128,128]{1,0:T(8,128)S(1)} %cholesky.688), custom_call_target="Cholesky" | custom-call | tf_op jit(solution)/shard_map/jit(cholesky)/cholesky | solution.py:13
  290.2 9.8 %custom-call.45 = f32[1,128,128]{1,2,0:T(8,128)S(1)} custom-call(f32[1,128,128]{2,1,0:T(8,128)S(1)} %get-tuple-element.81), custom_call_target="InvertDiagBlocksLowerTriangular" | custom-call | tf_op jit(solution)/shard_map/jit(cholesky)/cholesky | solution.py:13
  301.5 11.9 %cholesky.548 = f32[128,128]{1,0:T(8,128)S(1)} custom-call(f32[128,128]{1,0:T(8,128)S(1)} %convolution_subtract_fusion.15), custom_call_target="Cholesky" | custom-call | tf_op jit(solution)/shard_map/jit(cholesky)/cholesky | solution.py:13
  320.2 17.6 %while.4 = (s32[]{:T(128)}, f32[768,768]{1,0:T(8,128)}, s32[6,2]{0,1:T(2,128)S(1)}, f32[6,128,128]{2,1,0:T(8,128)S(1)}, s32[]{:T(128)}) while((s32[]{:T(128)}, f32[768,768]{1,0:T(8,128)}, s32[6,2]{0,1:T(2,128)S(1)}, f32[6,128,128]{2,1,0:T(8,128)S(1)}, s32[]{:T(128)}) %tuple.84), condition=%wide.while_cond, body=%wide.while_body.sunk | while | flops 2 | bytes 131189 | solution.py:14
  337.8 59.0 %custom-call.46 = f32[6,128,128]{1,2,0:T(8,128)S(1)} custom-call(f32[6,128,128]{2,1,0:T(8,128)S(1)} %get-tuple-element.18), custom_call_target="InvertDiagBlocksLowerTriangular" | custom-call | tf_op jit(solution)/shard_map/triangular_solve/custom-call.5 | solution.py:14
  416.5 5.8 convolution_subtract_fusion.3
  423.7 9.1 %fusion.143 = f32[768,768]{0,1:T(8,128)} fusion(f32[1024,768]{0,1:T(8,128)S(1)} %get-tuple-element.101), kind=kOutput, calls=%fused_computation.241 | convolution fusion | flops 7247757312 | bytes 5505024 | tf_op jit(solution)/shard_map/dot_general | solution.py:11
  432.9 150.4 %all-reduce.6.cloned.1.call-done = f32[768,768]{0,1:T(8,128)} async-done(((f32[768,768]{0,1:T(8,128)}), f32[768,768]{0,1:T(8,128)}) %all-reduce.6.cloned.1.call-update) | async-done | bytes 2359312 | tf_op jit(solution)/shard_map/psum | solution.py:12
  590.6 11.7 %cholesky.563 = f32[128,128]{1,0:T(8,128)S(1)} custom-call(f32[128,128]{1,0:T(8,128)S(1)} %cholesky.692), custom_call_target="Cholesky" | custom-call | tf_op jit(solution)/shard_map/jit(cholesky)/cholesky | solution.py:13
  603.6 10.6 %custom-call.47 = f32[1,128,128]{1,2,0:T(8,128)S(1)} custom-call(f32[1,128,128]{2,1,0:T(8,128)} %get-tuple-element.77), custom_call_target="InvertDiagBlocksLowerTriangular" | custom-call | tf_op jit(solution)/shard_map/jit(cholesky)/cholesky | solution.py:13
  620.0 11.7 %cholesky.582 = f32[128,128]{1,0:T(8,128)S(1)} custom-call(f32[128,128]{1,0:T(8,128)S(1)} %cholesky.696), custom_call_target="Cholesky" | custom-call | tf_op jit(solution)/shard_map/jit(cholesky)/cholesky | solution.py:13
  633.1 10.0 %custom-call.48 = f32[1,128,128]{1,2,0:T(8,128)S(1)} custom-call(f32[1,128,128]{2,1,0:T(8,128)S(1)} %get-tuple-element.74), custom_call_target="InvertDiagBlocksLowerTriangular" | custom-call | tf_op jit(solution)/shard_map/jit(cholesky)/cholesky | solution.py:13
  647.6 11.7 %cholesky.603 = f32[128,128]{1,0:T(8,128)S(1)} custom-call(f32[128,128]{1,0:T(8,128)S(1)} %cholesky.701), custom_call_target="Cholesky" | custom-call | tf_op jit(solution)/shard_map/jit(cholesky)/cholesky | solution.py:13
  660.6 9.8 %custom-call.49 = f32[1,128,128]{1,2,0:T(8,128)S(1)} custom-call(f32[1,128,128]{2,1,0:T(8,128)S(1)} %get-tuple-element.71), custom_call_target="InvertDiagBlocksLowerTriangular" | custom-call | tf_op jit(solution)/shard_map/jit(cholesky)/cholesky | solution.py:13
  674.8 12.1 %cholesky.622 = f32[128,128]{1,0:T(8,128)S(1)} custom-call(f32[128,128]{1,0:T(8,128)S(1)} %cholesky.706), custom_call_target="Cholesky" | custom-call | tf_op jit(solution)/shard_map/jit(cholesky)/cholesky | solution.py:13
  688.3 9.8 %custom-call.50 = f32[1,128,128]{1,2,0:T(8,128)S(1)} custom-call(f32[1,128,128]{2,1,0:T(8,128)S(1)} %get-tuple-element.68), custom_call_target="InvertDiagBlocksLowerTriangular" | custom-call | tf_op jit(solution)/shard_map/jit(cholesky)/cholesky | solution.py:13
  702.3 13.2 %cholesky.641 = f32[128,128]{1,0:T(8,128)} custom-call(f32[128,128]{1,0:T(8,128)} %cholesky.711), custom_call_target="Cholesky" | custom-call | tf_op jit(solution)/shard_map/jit(cholesky)/cholesky | solution.py:13
  717.6 11.3 %custom-call.51 = f32[1,128,128]{1,2,0:T(8,128)} custom-call(f32[1,128,128]{2,1,0:T(8,128)} %get-tuple-element.65), custom_call_target="InvertDiagBlocksLowerTriangular" | custom-call | tf_op jit(solution)/shard_map/jit(cholesky)/cholesky | solution.py:13
  732.1 11.9 %cholesky.658 = f32[128,128]{1,0:T(8,128)S(1)} custom-call(f32[128,128]{1,0:T(8,128)S(1)} %convolution_subtract_fusion.14), custom_call_target="Cholesky" | custom-call | tf_op jit(solution)/shard_map/jit(cholesky)/cholesky | solution.py:13
  749.0 13.8 %fusion.22 = f32[768,768]{1,0:T(8,128)} fusion(f32[768,768]{1,0:T(8,128)} %get-tuple-element.63, f32[768,768]{1,0:T(8,128)S(1)} %get-tuple-element.79, pred[]{:T(512)S(6)} %cholesky.663, pred[]{:T(512)S(6)} %cholesky.553), kind=kOutput, calls=%fused_computation.29 | convolution fusion | flops 5439356928 | bytes 7077890 | tf_op jit(solution)/shard_map/dot_general | solution.py:24
  765.4 15.5 %while.5 = (s32[]{:T(128)}, f32[768,768]{1,0:T(8,128)S(1)}, s32[6,2]{0,1:T(2,128)S(1)}, f32[6,128,128]{2,1,0:T(8,128)}, s32[]{:T(128)}) while((s32[]{:T(128)}, f32[768,768]{1,0:T(8,128)S(1)}, s32[6,2]{0,1:T(2,128)S(1)}, f32[6,128,128]{2,1,0:T(8,128)}, s32[]{:T(128)}) %tuple.94), condition=%wide.while_cond.clone, body=%wide.while_body.clone.sunk | while | flops 2 | bytes 132205 | solution.py:14
  782.3 60.6 %custom-call.52 = f32[6,128,128]{1,2,0:T(8,128)} custom-call(f32[6,128,128]{2,1,0:T(8,128)} %get-tuple-element.19), custom_call_target="InvertDiagBlocksLowerTriangular" | custom-call | tf_op jit(solution)/shard_map/triangular_solve/custom-call.5 | solution.py:14
  (161 shorter events, 141.6 us)
Async XLA Ops:
  7.2 167.0 %all-reduce.4.cloned.1.call-start = ((), (), s32[]{:S(2)}) async-start(), calls=%async_computation | async-start | bytes 4718592 | tf_op jit(solution)/shard_map/psum | solution.py:12
  18.8 564.5 %all-reduce.6.cloned.1.call-start = ((), (), s32[]{:S(2)}) async-start(), calls=%async_computation.1 | async-start | bytes 4718592 | tf_op jit(solution)/shard_map/psum | solution.py:12
  174.2 3.4 copy-start
  179.5 1.4 copy-start.2
  396.7 4.1 copy-start.15
  398.6 3.8 copy-start.6
  400.9 4.3 copy-start.16
  405.9 4.6 copy-start.4
  410.4 6.1 copy-start.8
  589.2 1.4 copy-start.1
  619.3 0.7 copy-start.10
  646.9 0.7 copy-start.11
  674.2 0.7 copy-start.12
  780.9 1.4 copy-start.3
  842.9 3.9 copy-start.14
  845.2 3.0 copy-start.5
  848.2 3.2 copy-start.9
  851.4 3.6 copy-start.13
  855.0 3.7 copy-start.7
Sparse Core Ops, SparseCore 0:
  18.9 155.2 all-reduce.3
  433.0 150.2 all-reduce.5
where the time goes:
time: 879 us; the launch traced here: 873 us
  other arithmetic  384 us (44%)
  waiting for transfers between devices  306 us (35%)
  matrix products  109 us (12%)
  local copies, waits for them, and re-layouts  52.5 us (6%)
  between operations  22.3 us (3%)
    psum x2, waiting for transfers between devices, sweep_local(): gram_mat = lax.psum(part_gram, GROUP_AXES)  306 us
    another operation x45, other arithmetic, sweep_local(): low_fac = jnp.linalg.cholesky(gram_mat)  256 us
    another operation x5, other arithmetic, sweep_local(): lax.linalg.triangular_solve(low_fac, row_blk, left_side=False, lower=True...  123 us
    another operation x22, matrix products, sweep_local(): lax.linalg.triangular_solve(low_fac, row_blk, left_side=False, lower=True...  46.7 us
    another operation x39, local copies, waits for them, and re-layouts, sweep_local(): lax.linalg.triangular_solve(low_fac, row_blk, left_side=False, lower=True...  33.8 us
    another operation x20, matrix products, sweep_local(): low_fac = jnp.linalg.cholesky(gram_mat)  27.7 us
    dot_general x2, matrix products, sweep_local(): lax.dot_general(row_blk, row_blk, (((0,), (0,)), ((), ())), precision=FUL...  20.7 us
  transfers between devices with their start and end apart: 2, of which 2 were waited for; matrix products, arithmetic and copies ran while one was open for 0% of the time, Pallas kernels for 0%

commit v1 on v0

v1 whole, which is shorter than its diff:
```python
import functools
import jax, jax.numpy as jnp
from jax import lax
from jax.experimental import pallas as pl
from jax.experimental.pallas import tpu as pltpu
from jax.sharding import PartitionSpec as P
MESH = pl.DeviceIdType.MESH
ROWS = 3072
HALF = 1536
NCH = 64
CH = 24

def ids():
    return lax.axis_index("outer"), lax.axis_index("rows")

def ar_direct(p_ref, o_ref, recv0, acc, recv1, red, s0, r0, s1, r1, s2, r2, s3, r3):
    c, me = ids()
    other = 1 - c
    bar = pltpu.get_barrier_semaphore()
    pl.semaphore_signal(bar, inc=1, device_id=(0, other, me), device_id_type=MESH)
    def sig(k, _):
        pl.semaphore_signal(bar, inc=1, device_id=(0, c, lax.rem(me + k, NCH)), device_id_type=MESH)
        return 0
    lax.fori_loop(1, NCH, sig, 0)
    pl.semaphore_wait(bar, NCH)
    cp = pltpu.make_async_remote_copy(p_ref.at[pl.ds(pl.multiple_of(other * HALF, 8), HALF)], recv0, s0, r0, device_id=(0, other, me), device_id_type=MESH)
    cp.start()
    cp.wait()
    acc[...] = p_ref[pl.ds(pl.multiple_of(c * HALF, 8), HALF)] + recv0[...]
    def mk1(k):
        peer = lax.rem(me + k, NCH)
        return pltpu.make_async_remote_copy(acc.at[pl.ds(pl.multiple_of(peer * CH, 8), CH)], recv1.at[pl.ds(pl.multiple_of((k - 1) * CH, 8), CH)], s1, r1, device_id=(0, c, peer), device_id_type=MESH)
    def st1(k, _):
        mk1(k).start()
        return 0
    lax.fori_loop(1, NCH, st1, 0)
    big = pltpu.make_async_remote_copy(acc.at[pl.ds(0, 63 * CH)], recv1, s1, r1, device_id=(0, c, me), device_id_type=MESH)
    big.wait_recv()
    tot = acc[pl.ds(pl.multiple_of(me * CH, 8), CH)]
    tot = lax.fori_loop(0, 63, lambda k, t: t + recv1[pl.ds(pl.multiple_of(k * CH, 8), CH)], tot)
    red[...] = tot
    off = pl.multiple_of(c * HALF + me * CH, 8)
    def st2(k, _):
        peer = lax.rem(me + k, NCH)
        pltpu.make_async_remote_copy(red, o_ref.at[pl.ds(off, CH)], s2, r2, device_id=(0, c, peer), device_id_type=MESH).start()
        return 0
    lax.fori_loop(1, NCH, st2, 0)
    o_ref[pl.ds(off, CH)] = tot
    big2 = pltpu.make_async_remote_copy(acc.at[pl.ds(0, 63 * CH)], recv1, s2, r2, device_id=(0, c, me), device_id_type=MESH)
    big2.wait_recv()
    half = pl.ds(pl.multiple_of(c * HALF, 8), HALF)
    cp3 = pltpu.make_async_remote_copy(o_ref.at[half], o_ref.at[half], s3, r3, device_id=(0, other, me), device_id_type=MESH)
    cp3.start()
    cp3.wait()
    big.wait_send()
    big2.wait_send()

def call_direct(p):
    return pl.pallas_call(
        ar_direct, out_shape=jax.ShapeDtypeStruct((ROWS, 128), jnp.float32),
        in_specs=[pl.BlockSpec(memory_space=pltpu.VMEM)], out_specs=pl.BlockSpec(memory_space=pltpu.VMEM),
        scratch_shapes=[pltpu.VMEM((HALF, 128), jnp.float32), pltpu.VMEM((HALF, 128), jnp.float32), pltpu.VMEM((63 * CH, 128), jnp.float32), pltpu.VMEM((CH, 128), jnp.float32)] + [pltpu.SemaphoreType.DMA] * 8,
        compiler_params=pltpu.CompilerParams(collective_id=0, has_side_effects=True), name="ar_direct")(p)


PAIRS = ((0, 0), (0, 1), (0, 2), (1, 1), (1, 2), (2, 2))
HI = lax.Precision.HIGHEST


def gram(x):
    blks = []
    for i, j in PAIRS:
        b = lax.dot_general(x[:, 256 * i:256 * i + 256], x[:, 256 * j:256 * j + 256], (((0,), (0,)), ((), ())), precision=HI, preferred_element_type=jnp.float32)
        blks += [b[:, :128], b[:, 128:]]
    s = call_direct(jnp.concatenate(blks, axis=0))
    full = {}
    for n, (i, j) in enumerate(PAIRS):
        b = jnp.concatenate([s[512 * n:512 * n + 256], s[512 * n + 256:512 * n + 512]], axis=1)
        full[i, j] = b
        if i != j:
            full[j, i] = b.T
    return jnp.concatenate([jnp.concatenate([full[i, j] for j in range(3)], axis=1) for i in range(3)], axis=0)


def sweep(x):
    low = jnp.linalg.cholesky(gram(x))
    return lax.linalg.triangular_solve(low, x, left_side=False, lower=True, transpose_a=True), low


def solution(mesh):
    spec = P(("batch", "outer", "rows"), None)

    def local_qr(a):
        q1, l1 = sweep(a)
        q2, l2 = sweep(q1)
        r = lax.dot_general(l2, l1, (((0,), (1,)), ((), ())), precision=HI, preferred_element_type=jnp.float32)
        return q2, r

    return jax.shard_map(local_qr, mesh=mesh, in_specs=(spec,), out_specs=(spec, P("batch", None)), check_vma=False)
```

time: 879 us -> 675 us (0.77)
  waiting for transfers between devices: 306 us -> 0 us
  Pallas kernels: 0 us -> 78.4 us
  local copies, waits for them, and re-layouts: 52.5 us -> 90.4 us
  between operations: 22.3 us -> 9.72 us
  matrix products: 109 us -> 96.9 us
    psum x2 -> x0, waiting for transfers between devices: 306 us -> none  [sweep_local(): gram_mat = lax.psum(part_gram, GROUP_AXES)]
    pallas_call x0 -> x2, Pallas kernels: none -> 78.4 us  [call_direct(): pl.pallas_call(ar_direct, out_shape=jax.ShapeDtypeStruct((ROWS, 128), jnp...]
    unnamed x35 -> x97, local copies, waits for them, and re-layouts: 9.84 us -> 39 us
    concatenate x0 -> x10, local copies, waits for them, and re-layouts: none -> 13.3 us  [the longest x6 7.23 us: gram(): jnp.concatenate([full[i, j] for j in range(3)], axis=1)]
    dot_general x3 -> x13, matrix products: 34.4 us -> 30.3 us  [the longest x12 20.5 us: gram(): lax.dot_general(x[:, 256 * i:256 * i + 256], x[:, 256 * j:256 * j + 256],...]
    another operation x50 -> x51, other arithmetic: 379 us -> 378 us  [the longest x46 254 us: sweep(): low = jnp.linalg.cholesky(gram(x))]
  transfers between devices with their start and end apart: 2 -> 0, of which waited for: 2 -> 0; matrix products, arithmetic and copies ran while one was open for 0% -> 0% of each run, Pallas kernels for 0% -> 0%
where the time goes in v1:
time: 675 us; the launch traced here: 664 us
  other arithmetic  388 us (57%)
  matrix products  96.9 us (14%)
  local copies, waits for them, and re-layouts  90.4 us (13%)
  Pallas kernels  78.4 us (12%)
  between operations  9.72 us (1%)
    another operation x46, other arithmetic, sweep(): low = jnp.linalg.cholesky(gram(x))  254 us
    another operation x5, other arithmetic, sweep(): lax.linalg.triangular_solve(low, x, left_side=False, lower=True, transpos...  124 us
    pallas_call x2, Pallas kernels, call_direct(): pl.pallas_call(ar_direct, out_shape=jax.ShapeDtypeStruct((ROWS, 128), jnp...  78.4 us
    another operation x22, matrix products, sweep(): lax.linalg.triangular_solve(low, x, left_side=False, lower=True, transpos...  41.7 us
    unnamed x97, local copies, waits for them, and re-layouts  39 us
    another operation x39, local copies, waits for them, and re-layouts, sweep(): lax.linalg.triangular_solve(low, x, left_side=False, lower=True, transpos...  34.6 us
    another operation x20, matrix products, sweep(): low = jnp.linalg.cholesky(gram(x))  24.9 us
    dot_general x12, matrix products, gram(): lax.dot_general(x[:, 256 * i:256 * i + 256], x[:, 256 * j:256 * j + 256],...  20.5 us

profile of v1, /device:TPU:1, one launch (start us, length us, event | category | flops | bytes accessed | tf_op | source)
XLA Modules:
  0.0 664.0 jit_solution(355079112656785523)
XLA Ops:
  22.9 42.4 %ar_direct.2 = f32[3072,128]{1,0:T(8,128)} custom-call(f32[3072,128]{1,0:T(8,128)} %slice_dynamic-update-slice_fusion.12.p_ref), custom_call_target="tpu_custom_call" | custom-call | tf_op jit(solution)/shard_map/ar_direct/pallas_call | solution.py:59
  100.2 11.7 %cholesky.453 = f32[128,128]{1,0:T(8,128)S(1)} custom-call(f32[128,128]{1,0:T(8,128)S(1)} %cholesky.669), custom_call_target="Cholesky" | custom-call | tf_op jit(solution)/shard_map/jit(cholesky)/cholesky | solution.py:86
  112.6 9.8 %custom-call.41 = f32[1,128,128]{1,2,0:T(8,128)S(1)} custom-call(f32[1,128,128]{2,1,0:T(8,128)S(1)} %get-tuple-element.105), custom_call_target="InvertDiagBlocksLowerTriangular" | custom-call | tf_op jit(solution)/shard_map/jit(cholesky)/cholesky | solution.py:86
  127.5 12.3 %cholesky.472 = f32[128,128]{1,0:T(8,128)} custom-call(f32[128,128]{1,0:T(8,128)S(1)} %cholesky.673), custom_call_target="Cholesky" | custom-call | tf_op jit(solution)/shard_map/jit(cholesky)/cholesky | solution.py:86
  143.3 10.6 %custom-call.42 = f32[1,128,128]{1,2,0:T(8,128)} custom-call(f32[1,128,128]{2,1,0:T(8,128)S(1)} %get-tuple-element.102), custom_call_target="InvertDiagBlocksLowerTriangular" | custom-call | tf_op jit(solution)/shard_map/jit(cholesky)/cholesky | solution.py:86
  157.6 11.7 %cholesky.493 = f32[128,128]{1,0:T(8,128)S(1)} custom-call(f32[128,128]{1,0:T(8,128)S(1)} %cholesky.678), custom_call_target="Cholesky" | custom-call | tf_op jit(solution)/shard_map/jit(cholesky)/cholesky | solution.py:86
  171.4 9.8 %custom-call.43 = f32[1,128,128]{1,2,0:T(8,128)S(1)} custom-call(f32[1,128,128]{2,1,0:T(8,128)S(1)} %get-tuple-element.99), custom_call_target="InvertDiagBlocksLowerTriangular" | custom-call | tf_op jit(solution)/shard_map/jit(cholesky)/cholesky | solution.py:86
  184.1 12.1 %cholesky.512 = f32[128,128]{1,0:T(8,128)S(1)} custom-call(f32[128,128]{1,0:T(8,128)S(1)} %cholesky.683), custom_call_target="Cholesky" | custom-call | tf_op jit(solution)/shard_map/jit(cholesky)/cholesky | solution.py:86
  198.3 9.8 %custom-call.44 = f32[1,128,128]{1,2,0:T(8,128)S(1)} custom-call(f32[1,128,128]{2,1,0:T(8,128)S(1)} %get-tuple-element.96), custom_call_target="InvertDiagBlocksLowerTriangular" | custom-call | tf_op jit(solution)/shard_map/jit(cholesky)/cholesky | solution.py:86
  210.8 11.7 %cholesky.531 = f32[128,128]{1,0:T(8,128)S(1)} custom-call(f32[128,128]{1,0:T(8,128)S(1)} %cholesky.688), custom_call_target="Cholesky" | custom-call | tf_op jit(solution)/shard_map/jit(cholesky)/cholesky | solution.py:86
  224.5 9.8 %custom-call.45 = f32[1,128,128]{1,2,0:T(8,128)S(1)} custom-call(f32[1,128,128]{2,1,0:T(8,128)S(1)} %get-tuple-element.93), custom_call_target="InvertDiagBlocksLowerTriangular" | custom-call | tf_op jit(solution)/shard_map/jit(cholesky)/cholesky | solution.py:86
  236.8 11.9 %cholesky.548 = f32[128,128]{1,0:T(8,128)S(1)} custom-call(f32[128,128]{1,0:T(8,128)S(1)} %convolution_subtract_fusion.15), custom_call_target="Cholesky" | custom-call | tf_op jit(solution)/shard_map/jit(cholesky)/cholesky | solution.py:86
  253.9 17.6 %while.4 = (s32[]{:T(128)}, f32[768,768]{1,0:T(8,128)}, s32[6,2]{0,1:T(2,128)S(1)}, f32[6,128,128]{2,1,0:T(8,128)S(1)}, s32[]{:T(128)}) while((s32[]{:T(128)}, f32[768,768]{1,0:T(8,128)}, s32[6,2]{0,1:T(2,128)S(1)}, f32[6,128,128]{2,1,0:T(8,128)S(1)}, s32[]{:T(128)}) %tuple.98), condition=%wide.while_cond, body=%wide.while_body.sunk | while | flops 2 | bytes 131189 | solution.py:87
  272.2 59.8 %custom-call.46 = f32[6,128,128]{1,2,0:T(8,128)S(1)} custom-call(f32[6,128,128]{2,1,0:T(8,128)} %copy-done.24), custom_call_target="InvertDiagBlocksLowerTriangular" | custom-call | tf_op jit(solution)/shard_map/triangular_solve/custom-call.5 | solution.py:87
  339.6 3.9 fusion.40
  346.2 4.9 fusion.46
  351.7 5.6 convolution_subtract_fusion.3
  362.5 35.9 %ar_direct.3 = f32[3072,128]{1,0:T(8,128)} custom-call(f32[3072,128]{1,0:T(8,128)} %copy-done.18), custom_call_target="tpu_custom_call" | custom-call | tf_op jit(solution)/shard_map/ar_direct/pallas_call | solution.py:59
  415.2 11.7 %cholesky.563 = f32[128,128]{1,0:T(8,128)S(1)} custom-call(f32[128,128]{1,0:T(8,128)S(1)} %cholesky.692), custom_call_target="Cholesky" | custom-call | tf_op jit(solution)/shard_map/jit(cholesky)/cholesky | solution.py:86
  427.6 9.8 %custom-call.47 = f32[1,128,128]{1,2,0:T(8,128)S(1)} custom-call(f32[1,128,128]{2,1,0:T(8,128)S(1)} %get-tuple-element.89), custom_call_target="InvertDiagBlocksLowerTriangular" | custom-call | tf_op jit(solution)/shard_map/jit(cholesky)/cholesky | solution.py:86
  440.4 11.7 %cholesky.582 = f32[128,128]{1,0:T(8,128)S(1)} custom-call(f32[128,128]{1,0:T(8,128)S(1)} %cholesky.696), custom_call_target="Cholesky" | custom-call | tf_op jit(solution)/shard_map/jit(cholesky)/cholesky | solution.py:86
  454.0 10.0 %custom-call.48 = f32[1,128,128]{1,2,0:T(8,128)S(1)} custom-call(f32[1,128,128]{2,1,0:T(8,128)S(1)} %get-tuple-element.86), custom_call_target="InvertDiagBlocksLowerTriangular" | custom-call | tf_op jit(solution)/shard_map/jit(cholesky)/cholesky | solution.py:86
  465.9 11.7 %cholesky.603 = f32[128,128]{1,0:T(8,128)S(1)} custom-call(f32[128,128]{1,0:T(8,128)S(1)} %cholesky.701), custom_call_target="Cholesky" | custom-call | tf_op jit(solution)/shard_map/jit(cholesky)/cholesky | solution.py:86
  479.0 9.8 %custom-call.49 = f32[1,128,128]{1,2,0:T(8,128)S(1)} custom-call(f32[1,128,128]{2,1,0:T(8,128)S(1)} %get-tuple-element.83), custom_call_target="InvertDiagBlocksLowerTriangular" | custom-call | tf_op jit(solution)/shard_map/jit(cholesky)/cholesky | solution.py:86
  490.7 12.1 %cholesky.622 = f32[128,128]{1,0:T(8,128)S(1)} custom-call(f32[128,128]{1,0:T(8,128)S(1)} %cholesky.706), custom_call_target="Cholesky" | custom-call | tf_op jit(solution)/shard_map/jit(cholesky)/cholesky | solution.py:86
  504.2 9.8 %custom-call.50 = f32[1,128,128]{1,2,0:T(8,128)S(1)} custom-call(f32[1,128,128]{2,1,0:T(8,128)S(1)} %get-tuple-element.80), custom_call_target="InvertDiagBlocksLowerTriangular" | custom-call | tf_op jit(solution)/shard_map/jit(cholesky)/cholesky | solution.py:86
  515.8 11.7 %cholesky.641 = f32[128,128]{1,0:T(8,128)S(1)} custom-call(f32[128,128]{1,0:T(8,128)S(1)} %cholesky.711), custom_call_target="Cholesky" | custom-call | tf_op jit(solution)/shard_map/jit(cholesky)/cholesky | solution.py:86
  528.9 9.8 %custom-call.51 = f32[1,128,128]{1,2,0:T(8,128)S(1)} custom-call(f32[1,128,128]{2,1,0:T(8,128)S(1)} %get-tuple-element.77), custom_call_target="InvertDiagBlocksLowerTriangular" | custom-call | tf_op jit(solution)/shard_map/jit(cholesky)/cholesky | solution.py:86
  540.2 11.9 %cholesky.658 = f32[128,128]{1,0:T(8,128)S(1)} custom-call(f32[128,128]{1,0:T(8,128)S(1)} %convolution_subtract_fusion.14), custom_call_target="Cholesky" | custom-call | tf_op jit(solution)/shard_map/jit(cholesky)/cholesky | solution.py:86
  553.4 9.8 %fusion.22 = f32[768,768]{1,0:T(8,128)} fusion(f32[768,768]{1,0:T(8,128)S(1)} %get-tuple-element.75, f32[768,768]{1,0:T(8,128)} %get-tuple-element.91, pred[]{:T(512)S(6)} %cholesky.663, pred[]{:T(512)S(6)} %cholesky.553), kind=kOutput, calls=%fused_computation.31 | convolution fusion | flops 5439356928 | bytes 7077890 | tf_op jit(solution)/shard_map/dot_general | solution.py:96
  564.9 17.2 %while.5 = (s32[]{:T(128)}, f32[768,768]{1,0:T(8,128)}, s32[6,2]{0,1:T(2,128)S(1)}, f32[6,128,128]{2,1,0:T(8,128)S(1)}, s32[]{:T(128)}) while((s32[]{:T(128)}, f32[768,768]{1,0:T(8,128)}, s32[6,2]{0,1:T(2,128)S(1)}, f32[6,128,128]{2,1,0:T(8,128)S(1)}, s32[]{:T(128)}) %tuple.104), condition=%wide.while_cond.clone, body=%wide.while_body.clone.sunk | while | flops 2 | bytes 131189 | solution.py:87
  582.1 59.2 %custom-call.52 = f32[6,128,128]{1,2,0:T(8,128)S(1)} custom-call(f32[6,128,128]{2,1,0:T(8,128)S(1)} %get-tuple-element.19), custom_call_target="InvertDiagBlocksLowerTriangular" | custom-call | tf_op jit(solution)/shard_map/triangular_solve/custom-call.5 | solution.py:87
  (249 shorter events, 191.3 us)
Async XLA Ops:
  0.6 6.9 %copy-start = (f32[1024,768]{1,0:T(8,128)S(1)}, f32[1024,768]{1,0:T(8,128)}, u32[]{:S(2)}) copy-start(f32[1024,768]{1,0:T(8,128)} %param.4) | copy-start | bytes 9437188
  75.6 9.1 %copy-start.21 = (f32[256,128]{1,0:T(8,128)}, f32[256,128]{1,0:T(8,128)S(1)}, u32[]{:S(2)}) copy-start(f32[256,128]{1,0:T(8,128)S(1)} %get-tuple-element.57) | copy-start | bytes 393220
  75.6 9.1 %copy-start.22 = (f32[256,128]{1,0:T(8,128)}, f32[256,128]{1,0:T(8,128)S(1)}, u32[]{:S(2)}) copy-start(f32[256,128]{1,0:T(8,128)S(1)} %get-tuple-element.58) | copy-start | bytes 393220
  85.4 5.1 copy-start.23
  85.4 6.0 copy-start.11
  85.4 6.0 copy-start.19
  86.7 3.9 copy-start.17
  90.6 0.9 copy-start.15
  98.8 1.4 copy-start.13
  271.5 0.7 copy-start.24
  332.6 25.3 %copy-start.1 = (f32[128,1024]{1,0:T(8,128)}, f32[128,1024]{1,0:T(8,128)S(1)}, u32[]{:S(2)}) copy-start(f32[128,1024]{1,0:T(8,128)S(1)} %get-tuple-element.109) | copy-start | bytes 1572868
  335.2 22.8 %copy-start.3 = (f32[1024,128]{0,1:T(8,128)}, f32[1024,128]{0,1:T(8,128)S(1)}, u32[]{:S(2)}) copy-start(f32[1024,128]{0,1:T(8,128)S(1)} %get-tuple-element.111) | copy-start | bytes 1572868
  339.6 19.4 %copy-start.5 = (f32[1024,128]{0,1:T(8,128)}, f32[1024,128]{0,1:T(8,128)S(1)}, u32[]{:S(2)}) copy-start(f32[1024,128]{0,1:T(8,128)S(1)} %get-tuple-element.113) | copy-start | bytes 1572868
  344.1 14.9 %copy-start.7 = (f32[1024,128]{0,1:T(8,128)}, f32[1024,128]{0,1:T(8,128)S(1)}, u32[]{:S(2)}) copy-start(f32[1024,128]{0,1:T(8,128)S(1)} %get-tuple-element.115) | copy-start | bytes 1572868
  351.7 8.4 %copy-start.9 = (f32[1024,128]{0,1:T(8,128)}, f32[1024,128]{0,1:T(8,128)S(1)}, u32[]{:S(2)}) copy-start(f32[1024,128]{0,1:T(8,128)S(1)} %get-tuple-element.117) | copy-start | bytes 1572868
  361.4 1.1 copy-start.18
  405.5 1.8 copy-start.12
  405.7 1.6 copy-start.20
  407.3 0.9 copy-start.16
  413.8 1.4 copy-start.14
  563.3 78.0 %copy-start.2 = (f32[128,1024]{1,0:T(8,128)S(1)}, f32[128,1024]{1,0:T(8,128)}, u32[]{:S(2)}) copy-start(f32[128,1024]{1,0:T(8,128)} %copy-done.1) | copy-start | bytes 1572868
  564.8 77.9 %copy-start.4 = (f32[1024,128]{0,1:T(8,128)S(1)}, f32[1024,128]{0,1:T(8,128)}, u32[]{:S(2)}) copy-start(f32[1024,128]{0,1:T(8,128)} %copy-done.3) | copy-start | bytes 1572868
  642.7 3.0 copy-start.6
  645.7 3.2 copy-start.8
  648.8 3.6 copy-start.10

commit v2 on v1

v2 whole, which is shorter than its diff:
```python
import functools
import jax
import jax.numpy as jnp
from jax import lax
from jax.experimental import pallas as pl
from jax.experimental.pallas import tpu as pltpu
from jax.sharding import PartitionSpec as P

MESH = pl.DeviceIdType.MESH
HI = lax.Precision.HIGHEST
N = 768
NB = 6
ROWS = 3072
HALF = 1536
NCH = 64
CH = 24
PAIRS = ((0, 0), (0, 1), (0, 2), (1, 1), (1, 2), (2, 2))


def dot(a, b, dims):
    return lax.dot_general(a, b, (dims, ((), ())), precision=HI, preferred_element_type=jnp.float32)


def m8(v):
    return pl.multiple_of(v, 8)


def unpack(s_ref, g):
    for n, (i, j) in enumerate(PAIRS):
        for h in range(2):
            g[256 * i:256 * i + 256, 256 * j + 128 * h:256 * j + 128 * h + 128] = s_ref[512 * n + 256 * h:512 * n + 256 * h + 256, :]


def bl(x, l):
    return jnp.broadcast_to(x[:, l:l + 1], (8, 128))

def bs(x, s):
    return jnp.broadcast_to(x[s:s + 1, :], (8, 128))

def factor(dref, uref, mref):
    sub = lax.broadcasted_iota(jnp.int32, (8, 128), 0)
    lane = lax.broadcasted_iota(jnp.int32, (8, 128), 1)
    zero = jnp.zeros((8, 128), jnp.float32)
    A = [dref[8 * i:8 * i + 8, :] for i in range(16)]
    for sp in range(8):
        l0 = 16 * sp
        ia, ib = 2 * sp, 2 * sp + 1
        blk = (lane >= l0) & (lane < l0 + 16)
        Ua, Ub = A[ia], A[ib]
        ca = [bl(Ua, l0 + s) for s in range(8)]
        cb = [bl(Ub, l0 + s) for s in range(16)]
        urg = [n for n in (ia + 2, ia + 3) if n < 16]
        cn = {n: [bl(A[n], l0 + s) for s in range(16)] for n in urg}
        Wa = jnp.where(blk, jnp.where(lane == sub + l0, 1.0, zero), Ua)
        Wb = jnp.where(blk, jnp.where(lane == sub + (l0 + 8), 1.0, zero), Ub)
        for n in range(ia + 2, 16):
            A[n] = jnp.where(blk, zero, A[n])
        for s in range(16):
            first = s < 8
            r = s % 8
            ri = lax.rsqrt(bs(ca[s] if first else cb[s], r))
            lb = cb[s] * ri
            if first:
                la = ca[s] * ri
                L = {t: (bs(la, t) if t < 8 else bs(lb, t - 8)) for t in range(s + 1, 16)}
                for t in range(s + 1, 8):
                    ca[t] = ca[t] - la * L[t]
                ma = jnp.where(sub > r, la, zero)
                u, w = bs(Ua, r) * ri, bs(Wa, r) * ri
                Ua = jnp.where(sub == r, u, Ua - ma * u)
                Wa = jnp.where(sub == r, w, Wa - ma * w)
                Ub = Ub - lb * u
                Wb = Wb - lb * w
            else:
                L = {t: bs(lb, t - 8) for t in range(s + 1, 16)}
                mb = jnp.where(sub > r, lb, zero)
                u, w = bs(Ub, r) * ri, bs(Wb, r) * ri
                Ub = jnp.where(sub == r, u, Ub - mb * u)
                Wb = jnp.where(sub == r, w, Wb - mb * w)
            for t in range(s + 1, 16):
                cb[t] = cb[t] - lb * L[t]
            for n in urg:
                ln = cn[n][s] * ri
                for t in range(s + 1, 16):
                    cn[n][t] = cn[n][t] - ln * L[t]
                A[n] = A[n] - ln * w
        uref[l0:l0 + 8, :] = jnp.where(lane >= sub + l0, Ua, zero)
        uref[l0 + 8:l0 + 16, :] = jnp.where(lane >= sub + (l0 + 8), Ub, zero)
        keep = lane < l0 + 16
        mref[l0:l0 + 8, :] = jnp.where(keep, Wa, zero)
        mref[l0 + 8:l0 + 16, :] = jnp.where(keep, Wb, zero)
        if ia + 4 < 16:
            W = jnp.concatenate([Wa, Wb], axis=0)
            D = dot(W, W, ((0,), (0,)))
            for n in range(ia + 4, 16):
                A[n] = A[n] - D[8 * n:8 * n + 8, :]


def chol_inv(g, u_ref, m_ref, dbuf, ubuf, mbuf):
    def step(k, _):
        for kk in range(NB):
            @pl.when(k == kk)
            def _():
                dbuf[...] = g[128 * kk:128 * kk + 128, 128 * kk:128 * kk + 128]
        factor(dbuf, ubuf, mbuf)
        for kk in range(NB):
            @pl.when(k == kk)
            def _():
                lo, hi = 128 * kk, 128 * kk + 128
                w = mbuf[...]
                u_ref[lo:hi, lo:hi] = ubuf[...]
                if kk > 0:
                    m_ref[lo:hi, :lo] = dot(w, m_ref[lo:hi, :lo], ((1,), (0,)))
                m_ref[lo:hi, lo:hi] = w
                if kk < NB - 1:
                    u_ref[lo:hi, hi:] = dot(w, g[lo:hi, hi:], ((1,), (0,)))
                    for i in range(kk + 1, NB):
                        a, b = 128 * i, 128 * i + 128
                        ut = u_ref[lo:hi, a:b]
                        g[a:b, a:] = g[a:b, a:] - dot(ut, u_ref[lo:hi, a:], ((0,), (0,)))
                        m_ref[a:b, :hi] = m_ref[a:b, :hi] - dot(ut, m_ref[lo:hi, :hi], ((0,), (0,)))
        return 0

    lax.fori_loop(0, NB, step, 0)


def apply_inv(x_ref, m_ref, q_ref):
    def rows(r, _):
        sl = pl.ds(pl.multiple_of(256 * r, 256), 256)
        for j in range(3):
            q_ref[sl, 256 * j:256 * j + 256] = dot(x_ref[sl, :256 * j + 256], m_ref[256 * j:256 * j + 256, :256 * j + 256], ((1,), (1,)))
        return 0
    lax.fori_loop(0, x_ref.shape[0] // 256, rows, 0)


def greet(c, me):
    bar = pltpu.get_barrier_semaphore()
    pl.semaphore_signal(bar, inc=1, device_id=(0, 1 - c, me), device_id_type=MESH)

    def sig(k, _):
        pl.semaphore_signal(bar, inc=1, device_id=(0, c, lax.rem(me + k, NCH)), device_id_type=MESH)
        return 0
    lax.fori_loop(1, NCH, sig, 0)
    return bar


def gram_half(x_ref, p_ref, half):
    def blk(t, _):
        n = 3 * half + t
        i = n // 3 + n // 5
        j = n - 2 * (n // 3) - n // 5
        b = dot(x_ref[:, pl.ds(pl.multiple_of(256 * i, 256), 256)], x_ref[:, pl.ds(pl.multiple_of(256 * j, 256), 256)], ((0,), (0,)))
        p_ref[pl.ds(m8(512 * n), 256), :] = b[:, :128]
        p_ref[pl.ds(m8(512 * n + 256), 256), :] = b[:, 128:]
        return 0
    lax.fori_loop(0, 3, blk, 0)


def gram_sum(bar, c, me, x_ref, p, o, recv0, acc, recv1, red, s0, r0, s1, r1, s2, r2, s3, r3):
    other = 1 - c
    gram_half(x_ref, p, other)
    pl.semaphore_wait(bar, NCH)
    mine = pl.ds(m8(c * HALF), HALF)
    cp = pltpu.make_async_remote_copy(p.at[pl.ds(m8(other * HALF), HALF)], recv0, s0, r0, device_id=(0, other, me), device_id_type=MESH)
    cp.start()
    gram_half(x_ref, p, c)
    cp.wait()
    acc[...] = p[mine] + recv0[...]

    def st1(k, _):
        peer = lax.rem(me + k, NCH)
        pltpu.make_async_remote_copy(acc.at[pl.ds(m8(peer * CH), CH)], recv1.at[pl.ds(m8((k - 1) * CH), CH)], s1, r1, device_id=(0, c, peer), device_id_type=MESH).start()
        return 0
    lax.fori_loop(1, NCH, st1, 0)
    big = pltpu.make_async_remote_copy(acc.at[pl.ds(0, 63 * CH)], recv1, s1, r1, device_id=(0, c, me), device_id_type=MESH)
    big.wait_recv()
    tot = lax.fori_loop(0, 63, lambda k, t: t + recv1[pl.ds(m8(k * CH), CH)], acc[pl.ds(m8(me * CH), CH)])
    red[...] = tot
    off = m8(c * HALF + me * CH)

    def st2(k, _):
        peer = lax.rem(me + k, NCH)
        pltpu.make_async_remote_copy(red, o.at[pl.ds(off, CH)], s2, r2, device_id=(0, c, peer), device_id_type=MESH).start()
        return 0
    lax.fori_loop(1, NCH, st2, 0)
    o[pl.ds(off, CH)] = tot
    big2 = pltpu.make_async_remote_copy(acc.at[pl.ds(0, 63 * CH)], recv1, s2, r2, device_id=(0, c, me), device_id_type=MESH)
    big2.wait_recv()
    cp3 = pltpu.make_async_remote_copy(o.at[mine], o.at[mine], s3, r3, device_id=(0, other, me), device_id_type=MESH)
    cp3.start()
    cp3.wait()
    big.wait_send()
    big2.wait_send()


def apply_inv(x_ref, m_ref, q_ref):
    def rows(r, _):
        sl = pl.ds(pl.multiple_of(256 * r, 256), 256)
        for j in range(3):
            q_ref[sl, 256 * j:256 * j + 256] = dot(x_ref[sl, :256 * j + 256], m_ref[256 * j:256 * j + 256, :256 * j + 256], ((1,), (1,)))
        return 0
    lax.fori_loop(0, x_ref.shape[0] // 256, rows, 0)


def clear(*refs):
    for r in refs:
        r[...] = jnp.zeros_like(r)


def first_kernel(x_ref, m_ref, u_ref, g, dbuf, ubuf, mbuf, *comm):
    c, me = lax.axis_index("outer"), lax.axis_index("rows")
    bar = greet(c, me)
    clear(m_ref, u_ref)
    gram_sum(bar, c, me, x_ref, *comm)
    unpack(comm[1], g)
    chol_inv(g, u_ref, m_ref, dbuf, ubuf, mbuf)


def second_kernel(x_ref, m1_ref, q_ref, m_ref, u_ref, g, dbuf, ubuf, mbuf, *comm):
    c, me = lax.axis_index("outer"), lax.axis_index("rows")
    bar = greet(c, me)
    clear(m_ref, u_ref)
    apply_inv(x_ref, m1_ref, q_ref)
    gram_sum(bar, c, me, q_ref, *comm)
    unpack(comm[1], g)
    chol_inv(g, u_ref, m_ref, dbuf, ubuf, mbuf)


def third_kernel(x_ref, m_ref, u2_ref, u1_ref, q_ref, r_ref):
    apply_inv(x_ref, m_ref, q_ref)
    for i in range(3):
        for j in range(3):
            a, b = slice(256 * i, 256 * i + 256), slice(256 * j, 256 * j + 256)
            if i > j:
                r_ref[a, b] = jnp.zeros((256, 256), jnp.float32)
            else:
                k = slice(256 * i, 256 * j + 256)
                r_ref[a, b] = dot(u2_ref[a, k], u1_ref[k, b], ((1,), (0,)))


NN = (N, N)
BUFS = [NN, (128, 128), (128, 128), (128, 128), (ROWS, 128), (ROWS, 128), (HALF, 128), (HALF, 128), (63 * CH, 128), (CH, 128)]


def vcall(kern, name, outs, args, cid=None):
    V = pl.BlockSpec(memory_space=pltpu.VMEM)
    scratch = [] if cid is None else [pltpu.VMEM(s, jnp.float32) for s in BUFS] + [pltpu.SemaphoreType.DMA] * 8
    params = {} if cid is None else dict(collective_id=cid, has_side_effects=True)
    return pl.pallas_call(
        kern, out_shape=tuple(jax.ShapeDtypeStruct(o, jnp.float32) for o in outs),
        in_specs=[V] * len(args), out_specs=(V,) * len(outs), scratch_shapes=scratch,
        compiler_params=pltpu.CompilerParams(vmem_limit_bytes=50 * 2**20, **params), name=name)(*args)


def solution(mesh):
    spec = P(("batch", "outer", "rows"), None)

    def local_qr(a):
        m1, u1 = vcall(first_kernel, "first", [NN, NN], [a], 0)
        q1, m2, u2 = vcall(second_kernel, "second", [a.shape, NN, NN], [a, m1], 1)
        return tuple(vcall(third_kernel, "third", [a.shape, NN], [q1, m2, u2, u1]))

    return jax.shard_map(local_qr, mesh=mesh, in_specs=(spec,), out_specs=(spec, P("batch", None)), check_vma=False)
```

time: 675 us -> 157 us (0.23); the launches traced: 664 us -> 157 us
  other arithmetic: 388 us -> 0 us
  matrix products: 96.9 us -> 0 us
  local copies, waits for them, and re-layouts: 90.4 us -> 1.4 us
  Pallas kernels: 78.4 us -> 155 us
  between operations: 9.72 us -> 0.65 us
    another operation x51 -> x0, other arithmetic: 378 us -> none  [the longest x46 254 us: sweep(): low = jnp.linalg.cholesky(gram(x))]
    pallas_call x2 -> x3, Pallas kernels: 78.4 us -> 155 us  [vcall(): pl.pallas_call(kern, out_shape=tuple((jax.ShapeDtypeStruct(o, jnp.float32...]
    another operation x42 -> x0, matrix products: 66.6 us -> none  [the longest x22 41.7 us: sweep(): lax.linalg.triangular_solve(low, x, left_side=False, lower=True, transpos...]
    unnamed x97 -> x2, local copies, waits for them, and re-layouts: 39 us -> 1.4 us
    another operation x51 -> x0, local copies, waits for them, and re-layouts: 36.4 us -> none  [the longest x39 34.6 us: sweep(): lax.linalg.triangular_solve(low, x, left_side=False, lower=True, transpos...]
    dot_general x13 -> x0, matrix products: 30.3 us -> none  [the longest x12 20.5 us: gram(): lax.dot_general(x[:, 256 * i:256 * i + 256], x[:, 256 * j:256 * j + 256],...]
    concatenate x10 -> x0, local copies, waits for them, and re-layouts: 13.3 us -> none  [the longest x6 7.23 us: gram(): jnp.concatenate([full[i, j] for j in range(3)], axis=1)]
where the time goes in v2:
time: 157 us
  Pallas kernels  155 us (99%)
    pallas_call x3, Pallas kernels, vcall(): pl.pallas_call(kern, out_shape=tuple((jax.ShapeDtypeStruct(o, jnp.float32...  155 us

profile of v2, /device:TPU:1, one launch (start us, length us, event | category | flops | bytes accessed | tf_op | source)
XLA Modules:
  0.0 157.1 jit_solution(2626617858124027109)
XLA Ops:
  0.6 68.7 %first.1 = (f32[768,768]{1,0:T(8,128)S(1)}, f32[768,768]{1,0:T(8,128)}) custom-call(f32[1024,768]{1,0:T(8,128)} %x_ref.3), custom_call_target="tpu_custom_call" | custom-call | tf_op jit(solution)/shard_map/first/pallas_call | solution.py:249
  69.3 0.0 copy-start
  69.3 1.4 copy-done
  70.7 73.1 %second.1 = (f32[1024,768]{1,0:T(8,128)}, f32[768,768]{1,0:T(8,128)S(1)}, f32[768,768]{1,0:T(8,128)}) custom-call(f32[1024,768]{1,0:T(8,128)} %x_ref.3, f32[768,768]{1,0:T(8,128)} %copy-done), custom_call_target="tpu_custom_call" | custom-call | tf_op jit(solution)/shard_map/second/pallas_call | solution.py:249
  143.8 13.3 %third.1 = (f32[1024,768]{1,0:T(8,128)}, f32[768,768]{1,0:T(8,128)}) custom-call(f32[1024,768]{1,0:T(8,128)} %get-tuple-element.8.x_ref, f32[768,768]{1,0:T(8,128)S(1)} %get-tuple-element.9.m_ref, f32[768,768]{1,0:T(8,128)} %get-tuple-element.10.u2_ref, f32[768,768]{1,0:T(8,128)} %get-tuple-element.11.u1_ref), custom_call_target="tpu_custom_call" | custom-call | tf_op jit(solution)/shard_map/third/pallas_call | solution.py:249
Async XLA Ops:
  69.3 1.4 copy-start
